TPU v7x, 32 devices: a whole 2x2x4 slice. The times are simulated.
32 devices in a mesh: row: 8 (over z, y), col: 4 (over x, core).
Axes of the slice: x: 2, y: 2, z: 4, core: 2. Of those that a mesh axis runs over, the one named last changes fastest.
Arguments:
- embeddings: bfloat16 [12288, 768], P(('row', 'col'))
- doc_order: int32 [12288], P(('row', 'col')), may hold values from 0 to 12287, each once
Outputs:
- nearest_earlier: float32 [12288], P(('row', 'col'))
Inputs may be any that keep to these rules, and one draw needn't show every extreme that they name: `doc_order`: each value 0 to 12287 appears once.
All inputs are finite; a program needn't handle non-finite values.
Results may differ from a plain program's by a relative error of at most 0.00051.
Values may be sent and summed in bfloat16 or wider, within the bound.
No kernel may reach another device: no remote copies, remote signals or barrier semaphores. Data moves between devices by JAX's collectives and lax.ppermute only.
A program may use at most 64 MiB of HBM per device.

v0:
```python
import jax
import jax.numpy as jnp
from jax import lax
from jax.sharding import PartitionSpec as P


def normalize_rows(embeddings):
    floats = embeddings.astype(jnp.float32)
    scale = lax.rsqrt(jnp.sum(floats * floats, axis=1, keepdims=True) + 1e-06)
    return (floats * scale).astype(jnp.bfloat16)


def block_size(length):
    width = min(512, length)
    while length % width != 0:
        width = width - 1
    return width


def masked_maxima(row_units, row_orders, col_units, col_orders, running):
    length = col_units.shape[0]
    width = block_size(length)
    col_groups = col_units.reshape(length // width, width, col_units.shape[1])
    order_groups = col_orders.reshape(length // width, width)

    def one_block(current, pair):
        units_here, orders_here = pair
        scores = jnp.dot(row_units, units_here.T, preferred_element_type=jnp.float32)
        earlier = orders_here[None, :] < row_orders[:, None]
        masked = jnp.where(earlier, scores, jnp.float32(-1.0))
        return (jnp.maximum(current, jnp.max(masked, axis=1)), None)

    result, unused = lax.scan(one_block, running, (col_groups, order_groups))
    return result


def shards(embeddings, doc_order):
    unit_rows = normalize_rows(embeddings)
    own_rows = unit_rows.shape[0]
    col_count = lax.axis_size("col")
    block_rows = own_rows * col_count
    initial = jnp.full((block_rows,), -1.0, jnp.float32)
    row_units, row_orders = (
        lax.all_gather(unit_rows, "col", axis=0, tiled=True),
        lax.all_gather(doc_order, "col", axis=0, tiled=True),
    )
    best_rows = masked_maxima(
        row_units,
        row_orders,
        lax.all_gather(unit_rows, "row", axis=0, tiled=True),
        lax.all_gather(doc_order, "row", axis=0, tiled=True),
        initial,
    )
    whole_max = lax.pmax(best_rows, "col")
    own_share = lax.dynamic_slice_in_dim(whole_max, lax.axis_index("col") * own_rows, own_rows, 0)
    return jnp.maximum(own_share, jnp.float32(-1.0))


def solution(mesh):
    return jax.shard_map(
        shards,
        mesh=mesh,
        in_specs=(P(("row", "col"), None), P(("row", "col"))),
        out_specs=P(("row", "col")),
        check_vma=False,
    )
```

profile of v0, /device:TPU:0, one launch (start us, length us, event | category | flops | bytes accessed | tf_op | source)
XLA Modules:
  0.0 152.0 jit_solution(297163370144080767)
XLA Ops:
  6.5 0.0 copy-start
  6.5 0.0 all-gather.7.cloned.1.call-start
  6.5 1.3 fusion.5
  7.8 2.0 %fusion.6 = bf16[384,768]{1,0:T(8,128)(2,1)} fusion(bf16[384,768]{1,0:T(8,128)(2,1)} %param.4, f32[384]{0:T(512)S(1)} %add_rsqrt_fusion), kind=kLoop, calls=%fused_computation.11 | loop fusion | flops 884736 | bytes 1181184 | tf_op jit(solution)/shard_map/convert_element_type | solution.py:10
  9.9 0.0 all-gather.7.cloned.1.call-update
  9.9 0.0 all-gather.5.cloned.1.call-start
  9.9 0.7 all-gather.5.cloned.1.call-update
  10.7 0.0 copy-done
  10.7 27.8 %all-gather = s32[8,1,384]{2,1,0:T(1,128)S(1)} all-gather(s32[1,1,384]{2,1,0:T(1,128)S(1)} %reshape.15), channel_id=1, replica_groups=mesh['row'=8,'col'=4] {'row'}, dimensions={0}, use_global_device_ids=true | all-gather | bytes 13824 | tf_op jit(solution)/shard_map/all_gather | solution.py:51
  38.6 5.2 %all-gather.1 = s32[4,1,384]{2,1,0:T(1,128)S(1)} all-gather(s32[1,1,384]{2,1,0:T(1,128)S(1)} %reshape.15), channel_id=1, replica_groups=mesh['row'=8,'col'=4] {'col'}, dimensions={0}, use_global_device_ids=true | all-gather | bytes 7680 | tf_op jit(solution)/shard_map/all_gather | solution.py:45
  43.8 0.0 all-gather.7.cloned.1.call-done
  43.8 74.5 %all-gather.5.cloned.1.call-done = bf16[3072,768]{1,0:T(8,128)(2,1)} async-done(((bf16[384,768]{1,0:T(8,128)(2,1)}), bf16[3072,768]{1,0:T(8,128)(2,1)}) %all-gather.5.cloned.1.call-update) | async-done | bytes 4718608 | tf_op jit(solution)/shard_map/all_gather | solution.py:50
  118.3 20.4 %while.11 = (s32[]{:T(128)}, f32[1536]{0:T(1024)S(1)}, s32[6,512]{1,0:T(8,128)S(1)}, s32[1536]{0:T(1024)S(1)}, bf16[6,512,768]{2,1,0:T(8,128)(2,1)}, /*index=5*/bf16[1536,768]{1,0:T(8,128)(2,1)}, s32[]{:T(128)}, s32[]{:T(128)}) while((s32[]{:T(128)}, f32[1536]{0:T(1024)S(1)}, s32[6,512]{1,0:T(8,128)S(1)}, s32[1536]{0:T(1024)S(1)}, ...), condition=%wide.region_3.4_spmd.clone, body=%wide.region_1.3_spmd.clone.sunk | while | flops 1210320384 | bytes 3183203 | solution.py:33
  118.4 3.3 %fusion.13 = f32[1536]{0:T(1024)S(1)} fusion(bf16[1536,768]{1,0:T(8,128)(2,1)} %get-tuple-element.129, s32[1536]{0:T(1024)S(1)} %get-tuple-element.127, s32[512]{0:T(512)S(1)} %bitcast.20, bf16[6,512,768]{2,1,0:T(8,128)(2,1)} %get-tuple-element.128, s32[]{:T(128)} %get-tuple-element.116), kind=kOutput, calls=%fused_computation.2.clone.1 | convolution fusion | flops 1210317312 | bytes 3160576 | tf_op jit(solution)/shard_map/while/body/eval_jaxpr/dot_general | solution.py:28
  121.8 3.3 %fusion.13 = f32[1536]{0:T(1024)S(1)} fusion(bf16[1536,768]{1,0:T(8,128)(2,1)} %get-tuple-element.129, s32[1536]{0:T(1024)S(1)} %get-tuple-element.127, s32[512]{0:T(512)S(1)} %bitcast.20, bf16[6,512,768]{2,1,0:T(8,128)(2,1)} %get-tuple-element.128, s32[]{:T(128)} %get-tuple-element.116), kind=kOutput, calls=%fused_computation.2.clone.1 | convolution fusion | flops 1210317312 | bytes 3160576 | tf_op jit(solution)/shard_map/while/body/eval_jaxpr/dot_general | solution.py:28
  125.2 3.3 %fusion.13 = f32[1536]{0:T(1024)S(1)} fusion(bf16[1536,768]{1,0:T(8,128)(2,1)} %get-tuple-element.129, s32[1536]{0:T(1024)S(1)} %get-tuple-element.127, s32[512]{0:T(512)S(1)} %bitcast.20, bf16[6,512,768]{2,1,0:T(8,128)(2,1)} %get-tuple-element.128, s32[]{:T(128)} %get-tuple-element.116), kind=kOutput, calls=%fused_computation.2.clone.1 | convolution fusion | flops 1210317312 | bytes 3160576 | tf_op jit(solution)/shard_map/while/body/eval_jaxpr/dot_general | solution.py:28
  128.6 3.3 %fusion.13 = f32[1536]{0:T(1024)S(1)} fusion(bf16[1536,768]{1,0:T(8,128)(2,1)} %get-tuple-element.129, s32[1536]{0:T(1024)S(1)} %get-tuple-element.127, s32[512]{0:T(512)S(1)} %bitcast.20, bf16[6,512,768]{2,1,0:T(8,128)(2,1)} %get-tuple-element.128, s32[]{:T(128)} %get-tuple-element.116), kind=kOutput, calls=%fused_computation.2.clone.1 | convolution fusion | flops 1210317312 | bytes 3160576 | tf_op jit(solution)/shard_map/while/body/eval_jaxpr/dot_general | solution.py:28
  132.0 3.3 %fusion.13 = f32[1536]{0:T(1024)S(1)} fusion(bf16[1536,768]{1,0:T(8,128)(2,1)} %get-tuple-element.129, s32[1536]{0:T(1024)S(1)} %get-tuple-element.127, s32[512]{0:T(512)S(1)} %bitcast.20, bf16[6,512,768]{2,1,0:T(8,128)(2,1)} %get-tuple-element.128, s32[]{:T(128)} %get-tuple-element.116), kind=kOutput, calls=%fused_computation.2.clone.1 | convolution fusion | flops 1210317312 | bytes 3160576 | tf_op jit(solution)/shard_map/while/body/eval_jaxpr/dot_general | solution.py:28
  135.4 3.3 %fusion.13 = f32[1536]{0:T(1024)S(1)} fusion(bf16[1536,768]{1,0:T(8,128)(2,1)} %get-tuple-element.129, s32[1536]{0:T(1024)S(1)} %get-tuple-element.127, s32[512]{0:T(512)S(1)} %bitcast.20, bf16[6,512,768]{2,1,0:T(8,128)(2,1)} %get-tuple-element.128, s32[]{:T(128)} %get-tuple-element.116), kind=kOutput, calls=%fused_computation.2.clone.1 | convolution fusion | flops 1210317312 | bytes 3160576 | tf_op jit(solution)/shard_map/while/body/eval_jaxpr/dot_general | solution.py:28
  138.7 5.8 %pmax.7 = f32[1536]{0:T(1024)S(1)} all-reduce(f32[1536]{0:T(1024)S(1)} %get-tuple-element.37), channel_id=1, replica_groups=mesh['row'=8,'col'=4] {'col'}, use_global_device_ids=true, to_apply=%region_4.5 | all-reduce | flops 1536 | bytes 12288 | tf_op jit(solution)/shard_map/pmax | solution.py:54
  144.5 0.7 dynamic-slice_maximum_fusion
  (19 shorter events, 0.2 us)
Async XLA Ops:
  6.5 4.1 %copy-start = (s32[384]{0:T(512)S(1)}, s32[384]{0:T(512)}, u32[]{:S(2)}) copy-start(s32[384]{0:T(512)} %param.5) | copy-start | bytes 4612
  6.5 37.3 %all-gather.7.cloned.1.call-start = ((), (), s32[]{:S(2)}) async-start(), calls=%async_computation.1 | async-start | bytes 2949120 | tf_op jit(solution)/shard_map/all_gather | solution.py:44
  9.9 108.5 %all-gather.5.cloned.1.call-start = ((), (), s32[]{:S(2)}) async-start(), calls=%async_computation | async-start | bytes 5308416 | tf_op jit(solution)/shard_map/all_gather | solution.py:50
Sparse Core Ops, SparseCore 0:
  10.0 26.7 all-gather.6
  39.0 79.3 all-gather.4
where the time goes:
time: 152 us
  waiting for transfers between devices  75.3 us (50%)
  blocking collectives  38.8 us (26%)
  matrix products  20.1 us (13%)
  between operations  13.5 us (9%)
  other arithmetic  4.08 us (3%)
    all_gather x1, waiting for transfers between devices, shards(): lax.all_gather(unit_rows, 'row', axis=0, tiled=True)  74.5 us
    all_gather x1, blocking collectives, shards(): lax.all_gather(doc_order, 'row', axis=0, tiled=True)  27.8 us
    dot_general x6, matrix products, one_block(): jnp.dot(row_units, units_here.T, preferred_element_type=jnp.float32)  20.1 us
    pmax x1, blocking collectives, shards(): whole_max = lax.pmax(best_rows, 'col')  5.77 us
    all_gather x1, blocking collectives, shards(): lax.all_gather(doc_order, 'col', axis=0, tiled=True)  5.18 us
  transfers between devices with their start and end apart: 2, of which 1 were waited for; matrix products, arithmetic and copies ran while one was open for 0% of the time, Pallas kernels for 0%

commit v1 on v0

--- a/solution.py
+++ b/solution.py
@@ -2,6 +2,36 @@
 import jax.numpy as jnp
 from jax import lax
 from jax.sharding import PartitionSpec as P
+
+
+def serve_circles(xin, dim_at):
+    xin = jnp.moveaxis(xin, 0, dim_at)
+    mixed_arr = xin.shape
+    return xin.reshape(
+        *mixed_arr[:dim_at], mixed_arr[dim_at] * mixed_arr[dim_at + 1], *mixed_arr[dim_at + 2 :]
+    )
+
+
+def _work_shifts_all(field_in, device_axis, pos_dim):
+    wide_n = lax.axis_size(device_axis)
+    table = [(dev_j, (dev_j + 1) % wide_n) for dev_j in range(wide_n)]
+    chunks = [(dd, hop_no) for hop_no, dd in table]
+    block_last, u_next = ([], [])
+    for q in range(wide_n - 1):
+        if q % 2 == 0:
+            block_last.append(
+                lax.ppermute(
+                    block_last[-1] if block_last else field_in, perm=table, axis_name=device_axis
+                )
+            )
+        else:
+            u_next.append(
+                lax.ppermute(u_next[-1] if u_next else field_in, perm=chunks, axis_name=device_axis)
+            )
+    odd = jnp.stack([*block_last[::-1], field_in, *u_next])
+    heard = lax.axis_index(device_axis) - len(block_last)
+    odd = odd[(jnp.arange(wide_n) - heard) % wide_n]
+    return serve_circles(odd, pos_dim)
 
 
 def normalize_rows(embeddings):
@@ -47,7 +77,7 @@
     best_rows = masked_maxima(
         row_units,
         row_orders,
-        lax.all_gather(unit_rows, "row", axis=0, tiled=True),
+        _work_shifts_all(unit_rows, "row", 0),
         lax.all_gather(doc_order, "row", axis=0, tiled=True),
         initial,
     )

time: 152 us -> 188 us (1.24)
  starting transfers between devices: 0.04 us -> 29.3 us
  waiting for transfers between devices: 75.3 us -> 52.7 us
  local copies, waits for them, and re-layouts: 0.07 us -> 19.5 us
  blocking collectives: 38.8 us -> 45.8 us
  other arithmetic: 4.08 us -> 6.32 us
    all_gather x1 -> x0, waiting for transfers between devices: 74.5 us -> none  [shards(): lax.all_gather(unit_rows, 'row', axis=0, tiled=True)]
    ppermute x0 -> x7, waiting for transfers between devices: none -> 52.6 us  [the longest x4 46.8 us: _work_shifts_all(): lax.ppermute(block_last[-1] if block_last else field_in, perm=table, axis...]
    ppermute x0 -> x7, starting transfers between devices: none -> 29.3 us  [the longest x3 21.3 us: _work_shifts_all(): lax.ppermute(u_next[-1] if u_next else field_in, perm=chunks, axis_name=d...]
    unnamed x4 -> x18, local copies, waits for them, and re-layouts: 0.02 us -> 7.61 us
    all_gather x1, blocking collectives: 27.8 us -> 33.9 us  [shards(): lax.all_gather(doc_order, 'row', axis=0, tiled=True)]
    gather x0 -> x1, local copies, waits for them, and re-layouts: none -> 5.31 us  [_work_shifts_all(): odd = odd[(jnp.arange(wide_n) - heard) % wide_n]]
    dynamic_slice x6, local copies, waits for them, and re-layouts: 0.05 us -> 4.36 us  [masked_maxima(): result, unused = lax.scan(one_block, running, (col_groups, order_groups))]
  transfers between devices with their start and end apart: 2 -> 8, of which waited for: 1 -> 4; matrix products, arithmetic and copies ran while one was open for 0% -> 10% of each run, Pallas kernels for 0% -> 0%
where the time goes in v1:
time: 188 us; the launch traced here: 187 us
  waiting for transfers between devices  52.7 us (28%)
  blocking collectives  45.8 us (24%)
  starting transfers between devices  29.3 us (16%)
  matrix products  20 us (11%)
  local copies, waits for them, and re-layouts  19.5 us (10%)
  between operations  13.5 us (7%)
  other arithmetic  6.32 us (3%)
    ppermute x4, waiting for transfers between devices, _work_shifts_all(): lax.ppermute(block_last[-1] if block_last else field_in, perm=table, axis...  46.8 us
    all_gather x1, blocking collectives, shards(): lax.all_gather(doc_order, 'row', axis=0, tiled=True)  33.9 us
    ppermute x3, starting transfers between devices, _work_shifts_all(): lax.ppermute(u_next[-1] if u_next else field_in, perm=chunks, axis_name=d...  21.3 us
    dot_general x6, matrix products, one_block(): jnp.dot(row_units, units_here.T, preferred_element_type=jnp.float32)  20 us
    ppermute x4, starting transfers between devices, _work_shifts_all(): lax.ppermute(block_last[-1] if block_last else field_in, perm=table, axis...  8.01 us
    unnamed x18, local copies, waits for them, and re-layouts  7.61 us
    pmax x1, blocking collectives, shards(): whole_max = lax.pmax(best_rows, 'col')  6.36 us
    ppermute x3, waiting for transfers between devices, _work_shifts_all(): lax.ppermute(u_next[-1] if u_next else field_in, perm=chunks, axis_name=d...  5.82 us
  transfers between devices with their start and end apart: 8, of which 4 were waited for; matrix products, arithmetic and copies ran while one was open for 10% of the time, Pallas kernels for 0%

profile of v1, /device:TPU:0, one launch (start us, length us, event | category | flops | bytes accessed | tf_op | source)
XLA Modules:
  0.0 187.3 jit_solution(13195945414176586034)
XLA Ops:
  6.5 0.0 copy-start
  6.5 0.0 all-gather.4.cloned.1.call-start
  6.5 1.3 fusion.5
  7.9 0.0 copy-start.2
  7.9 1.2 fusion.6
  9.1 0.0 copy-start.1
  9.1 3.0 %collective-permute-start = (bf16[384,768]{1,0:T(8,128)(2,1)S(1)}, bf16[384,768]{1,0:T(8,128)(2,1)S(1)}, u32[]{:S(2)}, u32[]{:S(2)}) collective-permute-start(bf16[384,768]{1,0:T(8,128)(2,1)S(1)} %fusion.6), channel_id=1, source_target_pairs={{0,4},{4,8},{8,12},{12,16},{16,20},{20,24},{24,28},{28,0},{1,5},{5... | collective-permute-start | bytes 1769480 | tf_op jit(solution)/shard_map/ppermute | solution.py:23
  12.2 16.4 %collective-permute-done = bf16[384,768]{1,0:T(8,128)(2,1)S(1)} collective-permute-done((bf16[384,768]{1,0:T(8,128)(2,1)S(1)}, bf16[384,768]{1,0:T(8,128)(2,1)S(1)}, u32[]{:S(2)}, u32[]{:S(2)}) %collective-permute-start) | collective-permute-done | bytes 589856 | tf_op jit(solution)/shard_map/ppermute | solution.py:23
  28.5 0.0 collective-permute-start.1
  28.5 0.0 copy-done.1
  28.5 0.0 all-gather.4.cloned.1.call-update
  28.6 4.8 %collective-permute-start.4 = (bf16[384,768]{1,0:T(8,128)(2,1)}, bf16[384,768]{1,0:T(8,128)(2,1)S(1)}, u32[]{:S(2)}, u32[]{:S(2)}) collective-permute-start(bf16[384,768]{1,0:T(8,128)(2,1)} %copy-done.1), channel_id=1, source_target_pairs={{4,0},{8,4},{12,8},{16,12},{20,16},{24,20},{28,24},{0,28},{5,1},{9... | collective-permute-start | bytes 1769480 | tf_op jit(solution)/shard_map/ppermute | solution.py:29
  33.3 20.1 %collective-permute-done.1 = bf16[384,768]{1,0:T(8,128)(2,1)S(1)} collective-permute-done((bf16[384,768]{1,0:T(8,128)(2,1)S(1)}, bf16[384,768]{1,0:T(8,128)(2,1)S(1)}, u32[]{:S(2)}, u32[]{:S(2)}) %collective-permute-start.1) | collective-permute-done | bytes 589856 | tf_op jit(solution)/shard_map/ppermute | solution.py:23
  53.5 2.5 %collective-permute-start.2 = (bf16[384,768]{1,0:T(8,128)(2,1)S(1)}, bf16[384,768]{1,0:T(8,128)(2,1)S(1)}, u32[]{:S(2)}, u32[]{:S(2)}) collective-permute-start(bf16[384,768]{1,0:T(8,128)(2,1)S(1)} %collective-permute-done.1), channel_id=1, source_target_pairs={{0,4},{4,8},{8,12},{12,16},{16,20},{20,24},{24,28},{28,0},{1,5},{5... | collective-permute-start | bytes 1769480 | tf_op jit(solution)/shard_map/ppermute | solution.py:23
  56.0 0.0 collective-permute-done.4
  56.0 13.7 %collective-permute-start.5 = (bf16[384,768]{1,0:T(8,128)(2,1)S(1)}, bf16[384,768]{1,0:T(8,128)(2,1)S(1)}, u32[]{:S(2)}, u32[]{:S(2)}) collective-permute-start(bf16[384,768]{1,0:T(8,128)(2,1)S(1)} %collective-permute-done.4), channel_id=1, source_target_pairs={{4,0},{8,4},{12,8},{16,12},{20,16},{24,20},{28,24},{0,28},{5,1},{9... | collective-permute-start | bytes 1769480 | tf_op jit(solution)/shard_map/ppermute | solution.py:29
  69.7 10.3 %collective-permute-done.2 = bf16[384,768]{1,0:T(8,128)(2,1)S(1)} collective-permute-done((bf16[384,768]{1,0:T(8,128)(2,1)S(1)}, bf16[384,768]{1,0:T(8,128)(2,1)S(1)}, u32[]{:S(2)}, u32[]{:S(2)}) %collective-permute-start.2) | collective-permute-done | bytes 589856 | tf_op jit(solution)/shard_map/ppermute | solution.py:23
  80.0 2.5 %collective-permute-start.3 = (bf16[384,768]{1,0:T(8,128)(2,1)S(1)}, bf16[384,768]{1,0:T(8,128)(2,1)}, u32[]{:S(2)}, u32[]{:S(2)}) collective-permute-start(bf16[384,768]{1,0:T(8,128)(2,1)S(1)} %collective-permute-done.2), channel_id=1, source_target_pairs={{0,4},{4,8},{8,12},{12,16},{16,20},{20,24},{24,28},{28,0},{1,5},{5... | collective-permute-start | bytes 1769480 | tf_op jit(solution)/shard_map/ppermute | solution.py:23
  82.5 0.0 copy-done.2
  82.5 0.7 reshape.68
  83.2 33.9 %all-gather = s32[8,1,384]{2,1,0:T(1,128)} all-gather(s32[1,1,384]{2,1,0:T(1,128)S(1)} %reshape.68), channel_id=1, replica_groups=mesh['row'=8,'col'=4] {'row'}, dimensions={0}, use_global_device_ids=true | all-gather | bytes 13824 | tf_op jit(solution)/shard_map/all_gather | solution.py:81
  117.1 1.3 reduce
  118.4 1.3 reshape.59
  119.7 5.6 %all-gather.1 = s32[4,1,384]{2,1,0:T(1,128)} all-gather(s32[1,1,384]{2,1,0:T(1,128)S(1)} %reshape.68), channel_id=1, replica_groups=mesh['row'=8,'col'=4] {'col'}, dimensions={0}, use_global_device_ids=true | all-gather | bytes 7680 | tf_op jit(solution)/shard_map/all_gather | solution.py:75
  125.3 0.7 reduce.1
  126.0 0.6 reshape.71
  126.7 0.0 copy-start.3
  126.7 0.0 collective-permute-done.5
  126.7 2.8 %collective-permute-start.6 = (bf16[384,768]{1,0:T(8,128)(2,1)S(1)}, bf16[384,768]{1,0:T(8,128)(2,1)S(1)}, u32[]{:S(2)}, u32[]{:S(2)}) collective-permute-start(bf16[384,768]{1,0:T(8,128)(2,1)S(1)} %collective-permute-done.5), channel_id=1, source_target_pairs={{4,0},{8,4},{12,8},{16,12},{20,16},{24,20},{28,24},{0,28},{5,1},{9... | collective-permute-start | bytes 1769480 | tf_op jit(solution)/shard_map/ppermute | solution.py:29
  129.5 0.0 collective-permute-done.3
  129.5 1.9 %bitcast_dynamic-update-slice_fusion.7 = bf16[8,384,768]{2,1,0:T(8,128)(2,1)} fusion(bf16[384,768]{1,0:T(8,128)(2,1)} %collective-permute-done.3), kind=kLoop, calls=%fused_computation.20 | loop fusion | bytes 1179648
  131.4 0.9 bitcast_dynamic-update-slice_fusion.6
  132.3 0.9 bitcast_dynamic-update-slice_fusion.5
  133.1 0.9 bitcast_dynamic-update-slice_fusion.4
  134.0 0.0 copy-done
  134.0 0.0 copy-done.3
  134.0 1.0 bitcast_dynamic-update-slice_fusion.3
  135.0 0.9 bitcast_dynamic-update-slice_fusion.2
  135.8 0.9 bitcast_dynamic-update-slice_fusion.1
  136.8 5.8 %collective-permute-done.6 = bf16[384,768]{1,0:T(8,128)(2,1)S(1)} collective-permute-done((bf16[384,768]{1,0:T(8,128)(2,1)S(1)}, bf16[384,768]{1,0:T(8,128)(2,1)S(1)}, u32[]{:S(2)}, u32[]{:S(2)}) %collective-permute-start.6) | collective-permute-done | bytes 589856 | tf_op jit(solution)/shard_map/ppermute | solution.py:29
  142.6 0.9 bitcast_dynamic-update-slice_fusion
  143.5 0.0 copy-start.4
  143.5 5.3 %gather_fusion = bf16[8,384,768]{2,1,0:T(8,128)(2,1)} fusion(bf16[8,384,768]{2,1,0:T(8,128)(2,1)} %bitcast_dynamic-update-slice_fusion, s32[1024]{0:T(1024)S(1)} %pad_clamp_fusion), kind=kCustom, calls=%fused_computation | custom fusion | bytes 9437216 | tf_op jit(solution)/shard_map/gather | solution.py:33
  148.8 0.0 all-gather.4.cloned.1.call-done
  148.8 0.0 copy-done.4
  148.8 24.6 %while.11 = (s32[]{:T(128)}, f32[1536]{0:T(1024)S(1)}, s32[6,512]{1,0:T(8,128)}, s32[1536]{0:T(1024)S(1)}, bf16[6,512,768]{2,1,0:T(8,128)(2,1)}, /*index=5*/bf16[1536,768]{1,0:T(8,128)(2,1)}, s32[]{:T(128)}, s32[]{:T(128)}) while((s32[]{:T(128)}, f32[1536]{0:T(1024)S(1)}, s32[6,512]{1,0:T(8,128)}, s32[1536]{0:T(1024)S(1)}, ...), condition=%wide.region_3.4_spmd.clone, body=%wide.region_1.3_spmd.clone.sunk | while | flops 1210320384 | bytes 3183203 | solution.py:63
  148.8 0.7 constant_dynamic-slice_fusion.2
  149.5 3.3 %fusion.15 = f32[1536]{0:T(1024)S(1)} fusion(bf16[1536,768]{1,0:T(8,128)(2,1)} %get-tuple-element.129, s32[1536]{0:T(1024)S(1)} %get-tuple-element.127, s32[512]{0:T(512)S(1)} %bitcast.39, bf16[6,512,768]{2,1,0:T(8,128)(2,1)} %get-tuple-element.128, s32[]{:T(128)} %get-tuple-element.116), kind=kOutput, calls=%fused_computation.3.clone.1 | convolution fusion | flops 1210317312 | bytes 3160576 | tf_op jit(solution)/shard_map/while/body/eval_jaxpr/dot_general | solution.py:58
  152.9 0.7 constant_dynamic-slice_fusion.2
  153.7 3.3 %fusion.15 = f32[1536]{0:T(1024)S(1)} fusion(bf16[1536,768]{1,0:T(8,128)(2,1)} %get-tuple-element.129, s32[1536]{0:T(1024)S(1)} %get-tuple-element.127, s32[512]{0:T(512)S(1)} %bitcast.39, bf16[6,512,768]{2,1,0:T(8,128)(2,1)} %get-tuple-element.128, s32[]{:T(128)} %get-tuple-element.116), kind=kOutput, calls=%fused_computation.3.clone.1 | convolution fusion | flops 1210317312 | bytes 3160576 | tf_op jit(solution)/shard_map/while/body/eval_jaxpr/dot_general | solution.py:58
  157.0 0.7 constant_dynamic-slice_fusion.2
  157.8 3.3 %fusion.15 = f32[1536]{0:T(1024)S(1)} fusion(bf16[1536,768]{1,0:T(8,128)(2,1)} %get-tuple-element.129, s32[1536]{0:T(1024)S(1)} %get-tuple-element.127, s32[512]{0:T(512)S(1)} %bitcast.39, bf16[6,512,768]{2,1,0:T(8,128)(2,1)} %get-tuple-element.128, s32[]{:T(128)} %get-tuple-element.116), kind=kOutput, calls=%fused_computation.3.clone.1 | convolution fusion | flops 1210317312 | bytes 3160576 | tf_op jit(solution)/shard_map/while/body/eval_jaxpr/dot_general | solution.py:58
  161.1 0.7 constant_dynamic-slice_fusion.2
  161.9 3.3 %fusion.15 = f32[1536]{0:T(1024)S(1)} fusion(bf16[1536,768]{1,0:T(8,128)(2,1)} %get-tuple-element.129, s32[1536]{0:T(1024)S(1)} %get-tuple-element.127, s32[512]{0:T(512)S(1)} %bitcast.39, bf16[6,512,768]{2,1,0:T(8,128)(2,1)} %get-tuple-element.128, s32[]{:T(128)} %get-tuple-element.116), kind=kOutput, calls=%fused_computation.3.clone.1 | convolution fusion | flops 1210317312 | bytes 3160576 | tf_op jit(solution)/shard_map/while/body/eval_jaxpr/dot_general | solution.py:58
  165.3 0.7 constant_dynamic-slice_fusion.2
  166.0 3.3 %fusion.15 = f32[1536]{0:T(1024)S(1)} fusion(bf16[1536,768]{1,0:T(8,128)(2,1)} %get-tuple-element.129, s32[1536]{0:T(1024)S(1)} %get-tuple-element.127, s32[512]{0:T(512)S(1)} %bitcast.39, bf16[6,512,768]{2,1,0:T(8,128)(2,1)} %get-tuple-element.128, s32[]{:T(128)} %get-tuple-element.116), kind=kOutput, calls=%fused_computation.3.clone.1 | convolution fusion | flops 1210317312 | bytes 3160576 | tf_op jit(solution)/shard_map/while/body/eval_jaxpr/dot_general | solution.py:58
  169.4 0.7 constant_dynamic-slice_fusion.2
  170.1 3.3 %fusion.15 = f32[1536]{0:T(1024)S(1)} fusion(bf16[1536,768]{1,0:T(8,128)(2,1)} %get-tuple-element.129, s32[1536]{0:T(1024)S(1)} %get-tuple-element.127, s32[512]{0:T(512)S(1)} %bitcast.39, bf16[6,512,768]{2,1,0:T(8,128)(2,1)} %get-tuple-element.128, s32[]{:T(128)} %get-tuple-element.116), kind=kOutput, calls=%fused_computation.3.clone.1 | convolution fusion | flops 1210317312 | bytes 3160576 | tf_op jit(solution)/shard_map/while/body/eval_jaxpr/dot_general | solution.py:58
  173.5 6.4 %pmax.7 = f32[1536]{0:T(1024)S(1)} all-reduce(f32[1536]{0:T(1024)S(1)} %get-tuple-element.37), channel_id=1, replica_groups=mesh['row'=8,'col'=4] {'col'}, use_global_device_ids=true, to_apply=%region_4.5 | all-reduce | flops 1536 | bytes 12288 | tf_op jit(solution)/shard_map/pmax | solution.py:84
  179.8 0.7 dynamic-slice_maximum_fusion
  (10 shorter events, 0.1 us)
Async XLA Ops:
  6.5 127.5 %copy-start = (bf16[384,768]{1,0:T(8,128)(2,1)S(1)}, bf16[384,768]{1,0:T(8,128)(2,1)}, u32[]{:S(2)}) copy-start(bf16[384,768]{1,0:T(8,128)(2,1)} %param.4) | copy-start | bytes 1769476
  6.5 142.3 %all-gather.4.cloned.1.call-start = ((), (), s32[]{:S(2)}) async-start(), calls=%async_computation | async-start | bytes 2949120 | tf_op jit(solution)/shard_map/all_gather | solution.py:74
  7.9 74.6 %copy-start.2 = (f32[384]{0:T(512)}, f32[384]{0:T(512)S(1)}, u32[]{:S(2)}) copy-start(f32[384]{0:T(512)S(1)} %add_rsqrt_fusion) | copy-start | bytes 4612
  9.1 19.4 %copy-start.1 = (bf16[384,768]{1,0:T(8,128)(2,1)}, bf16[384,768]{1,0:T(8,128)(2,1)S(1)}, u32[]{:S(2)}) copy-start(bf16[384,768]{1,0:T(8,128)(2,1)S(1)} %fusion.6) | copy-start | bytes 1769476
  9.1 19.4 %collective-permute-start = (bf16[384,768]{1,0:T(8,128)(2,1)S(1)}, bf16[384,768]{1,0:T(8,128)(2,1)S(1)}, u32[]{:S(2)}, u32[]{:S(2)}) collective-permute-start(bf16[384,768]{1,0:T(8,128)(2,1)S(1)} %fusion.6), channel_id=1, source_target_pairs={{0,4},{4,8},{8,12},{12,16},{16,20},{20,24},{24,28},{28,0},{1,5},{5... | collective-permute-start | bytes 1769480 | tf_op jit(solution)/shard_map/ppermute | solution.py:23
  28.5 24.9 %collective-permute-start.1 = (bf16[384,768]{1,0:T(8,128)(2,1)S(1)}, bf16[384,768]{1,0:T(8,128)(2,1)S(1)}, u32[]{:S(2)}, u32[]{:S(2)}) collective-permute-start(bf16[384,768]{1,0:T(8,128)(2,1)S(1)} %collective-permute-done), channel_id=1, source_target_pairs={{0,4},{4,8},{8,12},{12,16},{16,20},{20,24},{24,28},{28,0},{1,5},{5... | collective-permute-start | bytes 1769480 | tf_op jit(solution)/shard_map/ppermute | solution.py:23
  28.6 27.4 %collective-permute-start.4 = (bf16[384,768]{1,0:T(8,128)(2,1)}, bf16[384,768]{1,0:T(8,128)(2,1)S(1)}, u32[]{:S(2)}, u32[]{:S(2)}) collective-permute-start(bf16[384,768]{1,0:T(8,128)(2,1)} %copy-done.1), channel_id=1, source_target_pairs={{4,0},{8,4},{12,8},{16,12},{20,16},{24,20},{28,24},{0,28},{5,1},{9... | collective-permute-start | bytes 1769480 | tf_op jit(solution)/shard_map/ppermute | solution.py:29
  53.5 26.6 %collective-permute-start.2 = (bf16[384,768]{1,0:T(8,128)(2,1)S(1)}, bf16[384,768]{1,0:T(8,128)(2,1)S(1)}, u32[]{:S(2)}, u32[]{:S(2)}) collective-permute-start(bf16[384,768]{1,0:T(8,128)(2,1)S(1)} %collective-permute-done.1), channel_id=1, source_target_pairs={{0,4},{4,8},{8,12},{12,16},{16,20},{20,24},{24,28},{28,0},{1,5},{5... | collective-permute-start | bytes 1769480 | tf_op jit(solution)/shard_map/ppermute | solution.py:23
  56.0 70.7 %collective-permute-start.5 = (bf16[384,768]{1,0:T(8,128)(2,1)S(1)}, bf16[384,768]{1,0:T(8,128)(2,1)S(1)}, u32[]{:S(2)}, u32[]{:S(2)}) collective-permute-start(bf16[384,768]{1,0:T(8,128)(2,1)S(1)} %collective-permute-done.4), channel_id=1, source_target_pairs={{4,0},{8,4},{12,8},{16,12},{20,16},{24,20},{28,24},{0,28},{5,1},{9... | collective-permute-start | bytes 1769480 | tf_op jit(solution)/shard_map/ppermute | solution.py:29
  80.0 49.4 %collective-permute-start.3 = (bf16[384,768]{1,0:T(8,128)(2,1)S(1)}, bf16[384,768]{1,0:T(8,128)(2,1)}, u32[]{:S(2)}, u32[]{:S(2)}) collective-permute-start(bf16[384,768]{1,0:T(8,128)(2,1)S(1)} %collective-permute-done.2), channel_id=1, source_target_pairs={{0,4},{4,8},{8,12},{12,16},{16,20},{20,24},{24,28},{28,0},{1,5},{5... | collective-permute-start | bytes 1769480 | tf_op jit(solution)/shard_map/ppermute | solution.py:23
  126.7 7.4 %copy-start.3 = (f32[384]{0:T(512)S(1)}, f32[384]{0:T(512)}, u32[]{:S(2)}) copy-start(f32[384]{0:T(512)} %copy-done.2) | copy-start | bytes 4612
  126.7 15.9 %collective-permute-start.6 = (bf16[384,768]{1,0:T(8,128)(2,1)S(1)}, bf16[384,768]{1,0:T(8,128)(2,1)S(1)}, u32[]{:S(2)}, u32[]{:S(2)}) collective-permute-start(bf16[384,768]{1,0:T(8,128)(2,1)S(1)} %collective-permute-done.5), channel_id=1, source_target_pairs={{4,0},{8,4},{12,8},{16,12},{20,16},{24,20},{28,24},{0,28},{5,1},{9... | collective-permute-start | bytes 1769480 | tf_op jit(solution)/shard_map/ppermute | solution.py:29
  143.5 5.3 %copy-start.4 = (s32[1536]{0:T(1024)S(1)}, s32[1536]{0:T(1024)}, u32[]{:S(2)}) copy-start(s32[1536]{0:T(1024)} %reshape.71) | copy-start | bytes 18436
Sparse Core Ops, SparseCore 0:
  28.7 25.4 all-gather.3
